TPU v7x, 16 devices: a whole 2x2x2 slice. The times are simulated.
16 devices in a mesh: dp: 2 (over z), tp: 8 (over y, x, core).
Axes of the slice: x: 2, y: 2, z: 2, core: 2. Of those that a mesh axis runs over, the one named last changes fastest.
Arguments:
- x: bfloat16 [512, 1024], P('dp'), parts along dimension 0
- cache_len: int32 [512], P('dp'), parts along dimension 0
- k_cache: bfloat16 [2, 512, 16, 128, 64], P(None, 'dp', 'tp'), parts along dimension 1
- v_cache: bfloat16 [2, 512, 16, 128, 64], P(None, 'dp', 'tp'), parts along dimension 1
- norm_gain: float32 [2, 2, 1024], replicated
- norm_bias: float32 [2, 2, 1024], replicated
- w_qkv: bfloat16 [2, 1024, 3, 16, 64], P(None, None, None, 'tp')
- b_qkv: bfloat16 [2, 3, 16, 64], P(None, None, 'tp')
- w_out: bfloat16 [2, 16, 64, 1024], P(None, 'tp')
- b_out: bfloat16 [2, 1024], replicated
- w_up: bfloat16 [2, 1024, 4096], P(None, None, 'tp')
- b_up: bfloat16 [2, 4096], P(None, 'tp')
- w_down: bfloat16 [2, 4096, 1024], P(None, 'tp')
- b_down: bfloat16 [2, 1024], replicated
Outputs:
- output 1: bfloat16 [512, 1024], P('dp'), parts along dimension 0
- output 2: bfloat16 [2, 512, 16, 128, 64], P(None, 'dp', 'tp'), parts along dimension 1
- output 3: bfloat16 [2, 512, 16, 128, 64], P(None, 'dp', 'tp'), parts along dimension 1
There are 2 independent parts. A program takes and returns all parts, laid end to end along the dimension named above; an argument that names none is the same for every part.
All inputs are finite; a program needn't handle non-finite values.
Results may differ from a plain program's by a relative error of at most 0.0166085.
Values are sent between devices in bfloat16 or wider.
A program may use at most 1 GiB of HBM per device.

v0:
```python
import jax
import jax.numpy as jnp
from jax import lax
from jax.sharding import PartitionSpec as P

NORM_EPS = 1e-5


def layer_norm(vec, gain_vec, bias_vec):
    vec_f = vec.astype(jnp.float32)
    row_mean = jnp.mean(vec_f, axis=-1, keepdims=True)
    centered = vec_f - row_mean
    row_var = jnp.mean(centered * centered, axis=-1, keepdims=True)
    return (centered * lax.rsqrt(row_var + NORM_EPS) * gain_vec + bias_vec).astype(jnp.bfloat16)


def solution(mesh):
    cache_spec = P(None, 'dp', 'tp', None, None)
    in_specs = (P('dp', None), P('dp'), cache_spec, cache_spec, P(), P(),
                P(None, None, None, 'tp', None), P(None, None, 'tp', None),
                P(None, 'tp', None, None), P(), P(None, None, 'tp'), P(None, 'tp'),
                P(None, 'tp', None), P())
    out_specs = (P('dp', None), cache_spec, cache_spec)

    def local_step(x, cache_len, k_cache, v_cache, norm_gain, norm_bias, w_qkv, b_qkv, w_out, b_out, w_up, b_up, w_down, b_down):
        num_layers = k_cache.shape[0]
        smax = k_cache.shape[3]
        head_dim = k_cache.shape[4]
        slots = jnp.arange(smax)
        write_here = slots[None, None, :, None] == cache_len[:, None, None, None]
        visible = slots[None, None, :] <= cache_len[:, None, None]
        scale = head_dim ** -0.5
        k_layers = []
        v_layers = []
        for layer in range(num_layers):
            hidden = layer_norm(x, norm_gain[layer, 0], norm_bias[layer, 0])
            qkv_all = (jnp.einsum('bc,cthd->bthd', hidden, w_qkv[layer], preferred_element_type=jnp.float32) + b_qkv[layer].astype(jnp.float32)).astype(jnp.bfloat16)
            k_layer = jnp.where(write_here, qkv_all[:, 1, :, None, :], k_cache[layer])
            v_layer = jnp.where(write_here, qkv_all[:, 2, :, None, :], v_cache[layer])
            scores = jnp.einsum('bhd,bhjd->bhj', qkv_all[:, 0], k_layer, preferred_element_type=jnp.float32) * scale
            scores = jnp.where(visible, scores, -1e30)
            attn_prob = jax.nn.softmax(scores, axis=-1).astype(jnp.bfloat16)
            attended = jnp.einsum('bhj,bhjd->bhd', attn_prob, v_layer, preferred_element_type=jnp.float32).astype(jnp.bfloat16)
            attn_part = jnp.einsum('bhd,hdc->bc', attended, w_out[layer], preferred_element_type=jnp.float32).astype(jnp.bfloat16)
            attn_sum = lax.psum(attn_part, 'tp')
            x_mid = (x.astype(jnp.float32) + attn_sum.astype(jnp.float32) + b_out[layer].astype(jnp.float32)).astype(jnp.bfloat16)
            hidden_mlp = layer_norm(x_mid, norm_gain[layer, 1], norm_bias[layer, 1])
            up_act = jnp.maximum(jnp.dot(hidden_mlp, w_up[layer], preferred_element_type=jnp.float32) + b_up[layer].astype(jnp.float32), 0.0).astype(jnp.bfloat16)
            mlp_part = jnp.dot(up_act, w_down[layer], preferred_element_type=jnp.float32).astype(jnp.bfloat16)
            mlp_sum = lax.psum(mlp_part, 'tp')
            x = (x_mid.astype(jnp.float32) + mlp_sum.astype(jnp.float32) + b_down[layer].astype(jnp.float32)).astype(jnp.bfloat16)
            k_layers.append(k_layer)
            v_layers.append(v_layer)
        return x, jnp.stack(k_layers), jnp.stack(v_layers)

    return jax.shard_map(local_step, mesh=mesh, in_specs=in_specs, out_specs=out_specs, check_vma=False)
```

profile of v0, /device:TPU:1, one launch (start us, length us, event | category | flops | bytes accessed | tf_op | source)
XLA Modules:
  0.0 259.7 jit_solution(5931968448217005969)
XLA Ops:
  7.2 0.0 all-reduce.5.cloned.1.call-start
  7.2 1.2 convert_reduce_fusion.3
  8.4 1.3 fusion.56
  9.7 0.7 bitcast_convert_fusion.4
  10.4 0.8 fusion.158
  11.2 0.8 fusion.159
  12.0 0.8 iota_compare_fusion.1
  12.8 1.5 fusion.157
  14.4 1.6 fusion.80
  16.0 0.1 add_convert_fusion.1
  16.1 0.1 copy.25
  16.3 0.1 copy.26
  16.4 0.2 copy.33
  16.5 7.9 %fusion.7 = f32[256,2,1,128]{3,2,1,0:T(1,128)S(1)} fusion(bf16[256,2,64,1]{2,3,1,0:T(2,128)(2,1)S(1)} %copy.33, pred[256,128]{1,0:T(8,128)(4,1)S(1)} %get-tuple-element.40, bf16[2,256,2,128,64]{3,4,2,1,0:T(8,128)(2,1)} %param.16, bf16[256,2,64]{2,1,0:T(2,128)(2,1)S(1)} %copy.25), kind=kOutput, calls=%fused_computation.13 | convolution fusion | flops 12582912 | bytes 8814592 | tf_op jit(solution)/shard_map/bhd,bhjd->bhj/dot_general | solution.py:40
  24.4 0.2 fusion.42
  24.7 0.0 copy-start.1
  24.7 0.0 copy-start.4
  24.7 0.0 copy-start.2
  24.7 0.0 copy-start
  24.7 8.0 %fusion.6 = bf16[256,2,1,64]{3,2,1,0:T(2,128)(2,1)S(1)} fusion(pred[256,128]{1,0:T(8,128)(4,1)S(1)} %get-tuple-element.40, bf16[2,256,2,128,64]{3,4,2,1,0:T(8,128)(2,1)} %param.17, bf16[256,2,64]{2,1,0:T(2,128)(2,1)S(1)} %copy.26, bf16[256,2,128,1]{2,0,1,3:T(8,128)(2,1)S(1)} %fusion.42), kind=kOutput, calls=%fused_computation.11 | convolution fusion | flops 12582912 | bytes 8683520 | tf_op jit(solution)/shard_map/bhj,bhjd->bhd/dot_general | solution.py:43
  32.7 0.0 copy-start.3
  32.7 0.1 copy.36
  32.9 0.0 copy-done.1
  32.9 1.1 fusion.20
  34.0 0.0 all-reduce.5.cloned.1.call-update
  34.0 0.0 all-reduce.7.cloned.1.call-start
  34.0 0.0 copy-done.4
  34.1 0.0 copy-done.2
  34.1 48.0 %all-reduce.5.cloned.1.call-done = bf16[256,1024]{1,0:T(8,128)(2,1)} async-done(((bf16[256,1024]{1,0:T(8,128)(2,1)}), bf16[256,1024]{1,0:T(8,128)(2,1)}) %all-reduce.5.cloned.1.call-update) | async-done | bytes 524304 | tf_op jit(solution)/shard_map/psum | solution.py:45
  82.1 0.0 copy-done
  82.2 1.3 convert_reduce_fusion.2
  83.5 0.3 fusion.52
  83.8 3.2 %convolution_convert_fusion.1 = bf16[256,1024]{1,0:T(8,128)(2,1)} fusion(bf16[2,512,1024]{2,1,0:T(8,128)(2,1)} %param.26, bf16[2,1024,512]{2,1,0:T(8,128)(2,1)} %param.24, bf16[256,1024]{1,0:T(8,128)(2,1)S(1)} %get-tuple-element.8, f32[1024]{0:T(1024)S(1)} %bitcast.127, f32[1024]{0:T(1024)S(1)} %bitcast.126, f32[256]{0:T(256)S(1)} %add_rsqrt_fusion.2, ...), kind=kOutput, calls=%fused_computation.47 | convolution fusion | flops 539099136 | bytes 3158016 | tf_op jit(solution)/shard_map/dot_general | solution.py:49
  87.0 0.0 all-reduce.7.cloned.1.call-update
  87.0 0.0 all-reduce.9.cloned.1.call-start
  87.0 0.0 copy-done.3
  87.1 46.3 %all-reduce.7.cloned.1.call-done = bf16[256,1024]{1,0:T(8,128)(2,1)} async-done(((bf16[256,1024]{1,0:T(8,128)(2,1)}), bf16[256,1024]{1,0:T(8,128)(2,1)}) %all-reduce.7.cloned.1.call-update) | async-done | bytes 524304 | tf_op jit(solution)/shard_map/psum | solution.py:50
  133.4 1.3 convert_reduce_fusion.1
  134.7 0.3 fusion.48
  135.0 0.5 fusion.84
  135.6 0.1 add_convert_fusion
  135.7 0.1 copy.27
  135.8 0.1 copy.28
  136.0 0.2 copy.37
  136.1 7.9 %fusion.5 = f32[256,2,1,128]{3,2,1,0:T(1,128)S(1)} fusion(bf16[256,2,64,1]{2,3,1,0:T(2,128)(2,1)S(1)} %copy.37, pred[256,128]{1,0:T(8,128)(4,1)S(1)} %get-tuple-element.40, bf16[2,256,2,128,64]{3,4,2,1,0:T(8,128)(2,1)} %param.16, bf16[256,2,64]{2,1,0:T(2,128)(2,1)S(1)} %copy.27), kind=kOutput, calls=%fused_computation.9 | convolution fusion | flops 12582912 | bytes 8814592 | tf_op jit(solution)/shard_map/bhd,bhjd->bhj/dot_general | solution.py:40
  144.0 0.2 fusion.43
  144.3 7.9 %fusion.4 = bf16[256,2,1,64]{3,2,1,0:T(2,128)(2,1)S(1)} fusion(pred[256,128]{1,0:T(8,128)(4,1)S(1)} %get-tuple-element.40, bf16[2,256,2,128,64]{3,4,2,1,0:T(8,128)(2,1)} %param.17, bf16[256,2,64]{2,1,0:T(2,128)(2,1)S(1)} %copy.28, bf16[256,2,128,1]{2,0,1,3:T(8,128)(2,1)S(1)} %fusion.43), kind=kOutput, calls=%fused_computation.7 | convolution fusion | flops 12582912 | bytes 8683520 | tf_op jit(solution)/shard_map/bhj,bhjd->bhd/dot_general | solution.py:43
  152.2 0.1 copy.40
  152.3 1.1 fusion.21
  153.4 0.0 all-reduce.9.cloned.1.call-update
  153.4 0.0 all-reduce.11.cloned.1.call-start
  153.5 22.8 %broadcast_select_fusion.1 = (bf16[1,256,2,128,64]{3,4,2,1,0:T(8,128)(2,1)}, bf16[1,256,2,128,64]{3,4,2,1,0:T(8,128)(2,1)}, bf16[1,256,2,128,64]{3,4,2,1,0:T(8,128)(2,1)}, bf16[1,256,2,128,64]{3,4,2,1,0:T(8,128)(2,1)}) fusion(pred[256,128]{1,0:T(8,128)(4,1)S(1)} %get-tuple-element.40, bf16[2,256,2,128,64]{3,4,2,1,0:T(8,128)(2,1)} %param.17, ...), kind=kLoop, calls=%fused_computation.15 | loop fusion | flops 16777216 | bytes 67403776 | tf_op jit(solution)/shard_map/jit(_where)/select_n | solution.py:39
  176.3 23.6 %all-reduce.9.cloned.1.call-done = bf16[256,1024]{1,0:T(8,128)(2,1)} async-done(((bf16[256,1024]{1,0:T(8,128)(2,1)}), bf16[256,1024]{1,0:T(8,128)(2,1)}) %all-reduce.9.cloned.1.call-update) | async-done | bytes 524304 | tf_op jit(solution)/shard_map/psum | solution.py:45
  199.9 1.3 convert_reduce_fusion
  201.2 0.3 fusion.44
  201.5 3.2 %convolution_convert_fusion = bf16[256,1024]{1,0:T(8,128)(2,1)} fusion(bf16[2,512,1024]{2,1,0:T(8,128)(2,1)} %param.26, bf16[2,1024,512]{2,1,0:T(8,128)(2,1)} %param.24, bf16[256,1024]{1,0:T(8,128)(2,1)S(1)} %get-tuple-element.4, f32[1024]{0:T(1024)S(1)} %bitcast.123, f32[1024]{0:T(1024)S(1)} %bitcast.122, f32[256]{0:T(256)S(1)} %add_rsqrt_fusion, ...), kind=kOutput, calls=%fused_computation.46 | convolution fusion | flops 539099136 | bytes 3158016 | tf_op jit(solution)/shard_map/dot_general | solution.py:49
  204.7 0.0 all-reduce.11.cloned.1.call-update
  204.7 22.8 %pad_maximum_fusion = (bf16[2,256,2,128,64]{3,4,2,1,0:T(8,128)(2,1)}, bf16[2,256,2,128,64]{3,4,2,1,0:T(8,128)(2,1)}) fusion(bf16[1,256,2,128,64]{3,4,2,1,0:T(8,128)(2,1)} %get-tuple-element.21, bf16[1,256,2,128,64]{3,4,2,1,0:T(8,128)(2,1)} %get-tuple-element.22, bf16[1,256,2,128,64]{3,4,2,1,0:T(8,128)(2,1)} %get-tuple-element.10, ...), kind=kLoop, calls=%fused_computation.4 | loop fusion | flops 16777216 | bytes 67108864 | tf_op jit(solution)/shard_map/stack | solution.py:54
  227.5 23.6 %all-reduce.11.cloned.1.call-done = bf16[256,1024]{1,0:T(8,128)(2,1)} async-done(((bf16[256,1024]{1,0:T(8,128)(2,1)}), bf16[256,1024]{1,0:T(8,128)(2,1)}) %all-reduce.11.cloned.1.call-update) | async-done | bytes 524304 | tf_op jit(solution)/shard_map/psum | solution.py:50
  251.1 2.0 fusion.67
  (13 shorter events, 0.1 us)
Async XLA Ops:
  7.2 75.0 %all-reduce.5.cloned.1.call-start = ((), (), s32[]{:S(2)}) async-start(), calls=%async_computation | async-start | bytes 1048576 | tf_op jit(solution)/shard_map/psum | solution.py:45
  24.7 8.2 %copy-start.1 = (bf16[2,2,64,1024]{3,2,1,0:T(8,128)(2,1)S(1)}, bf16[2,2,64,1024]{3,2,1,0:T(8,128)(2,1)}, u32[]{:S(2)}) copy-start(bf16[2,2,64,1024]{3,2,1,0:T(8,128)(2,1)} %param.22) | copy-start | bytes 1572868
  24.7 9.4 %copy-start.4 = (bf16[2,512]{1,0:T(2,128)(2,1)S(1)}, bf16[2,512]{1,0:T(2,128)(2,1)}, u32[]{:S(2)}) copy-start(bf16[2,512]{1,0:T(2,128)(2,1)} %param.25) | copy-start | bytes 6148
  24.7 9.4 %copy-start.2 = (bf16[2,1024]{1,0:T(2,128)(2,1)S(1)}, bf16[2,1024]{1,0:T(2,128)(2,1)}, u32[]{:S(2)}) copy-start(bf16[2,1024]{1,0:T(2,128)(2,1)} %param.23) | copy-start | bytes 12292
  24.7 57.4 %copy-start = (bf16[256,1024]{1,0:T(8,128)(2,1)S(1)}, bf16[256,1024]{1,0:T(8,128)(2,1)}, u32[]{:S(2)}) copy-start(bf16[256,1024]{1,0:T(8,128)(2,1)} %param.14) | copy-start | bytes 1572868
  32.7 54.3 %copy-start.3 = (bf16[2,1024]{1,0:T(2,128)(2,1)S(1)}, bf16[2,1024]{1,0:T(2,128)(2,1)}, u32[]{:S(2)}) copy-start(bf16[2,1024]{1,0:T(2,128)(2,1)} %param.27) | copy-start | bytes 12292
  34.0 99.4 %all-reduce.7.cloned.1.call-start = ((), (), s32[]{:S(2)}) async-start(), calls=%async_computation.1 | async-start | bytes 1048576 | tf_op jit(solution)/shard_map/psum | solution.py:50
  87.0 112.9 %all-reduce.9.cloned.1.call-start = ((), (), s32[]{:S(2)}) async-start(), calls=%async_computation.2 | async-start | bytes 1048576 | tf_op jit(solution)/shard_map/psum | solution.py:45
  153.4 97.7 %all-reduce.11.cloned.1.call-start = ((), (), s32[]{:S(2)}) async-start(), calls=%async_computation.3 | async-start | bytes 1048576 | tf_op jit(solution)/shard_map/psum | solution.py:50
Sparse Core Ops, SparseCore 0:
  34.1 47.9 all-reduce.4
  87.1 46.2 all-reduce.6
  153.6 46.2 all-reduce.8
  204.8 46.2 all-reduce.10
where the time goes:
time: 263 us; the launch traced here: 260 us
  waiting for transfers between devices  142 us (54%)
  other arithmetic  57.2 us (22%)
  matrix products  42.4 us (16%)
  between operations  14 us (5%)
  local copies, waits for them, and re-layouts  4.21 us (2%)
    psum x2, waiting for transfers between devices, local_step(): attn_sum = lax.psum(attn_part, 'tp')  71.7 us
    psum x2, waiting for transfers between devices, local_step(): mlp_sum = lax.psum(mlp_part, 'tp')  70 us
    another operation x1, other arithmetic, local_step(): return (x, jnp.stack(k_layers), jnp.stack(v_layers))  22.8 us
    select_n x1, other arithmetic, local_step(): v_layer = jnp.where(write_here, qkv_all[:, 2, :, None, :], v_cache[layer])  22.8 us
    dot_general x2, matrix products, local_step(): jnp.einsum('bhj,bhjd->bhd', attn_prob, v_layer, preferred_element_type=jn...  15.9 us
    dot_general x2, matrix products, local_step(): jnp.einsum('bhd,bhjd->bhj', qkv_all[:, 0], k_layer, preferred_element_typ...  15.8 us
    dot_general x2, matrix products, local_step(): jnp.dot(up_act, w_down[layer], preferred_element_type=jnp.float32)  6.38 us
  transfers between devices with their start and end apart: 4, of which 4 were waited for; matrix products, arithmetic and copies ran while one was open for 18% of the time, Pallas kernels for 0%

commit v1 on v0

v1 whole, which is shorter than its diff:
```python
import functools

import jax
import jax.numpy as jnp
from jax import lax
from jax.experimental import pallas as pl
from jax.experimental.pallas import tpu as pltpu
from jax.sharding import PartitionSpec as P

F32 = jnp.float32
BF16 = jnp.bfloat16
EPS = 1e-5
MESH = pl.DeviceIdType.MESH
GB = 16


def norm_rows(xf, gain, bias):
    mean = jnp.mean(xf, axis=-1, keepdims=True)
    cen = xf - mean
    var = jnp.mean(cen * cen, axis=-1, keepdims=True)
    return (cen * lax.rsqrt(var + EPS) * gain + bias).astype(BF16)


def nt_dot(a, b):
    return lax.dot_general(a, b, (((1,), (1,)), ((), ())), preferred_element_type=F32)


def attn_kernel(layer, aliased, len_ref, gain_ref, bias_ref, bq_ref, x_hbm, w_hbm, k_hbm, v_hbm, *rest):
    if aliased:
        rest = rest[2:]
    k_out, v_out, a_ref, x_s, w_s, k_s, v_s, q_s, kvt_s, p_s, in_sem, out_sem, xw_sem = rest
    nb = x_s.shape[0]
    hd = 128
    smax = 128
    groups = nb // GB

    def rows(g):
        return pl.ds(pl.multiple_of(g * GB, GB), GB)

    def load(g):
        return [pltpu.make_async_copy(hbm.at[layer, rows(g)], buf.at[rows(g)], in_sem.at[t, g])
                for t, (hbm, buf) in enumerate(((k_hbm, k_s), (v_hbm, v_s)))]

    def save(g):
        return [pltpu.make_async_copy(buf.at[rows(g)], hbm.at[layer, rows(g)], out_sem.at[t, g])
                for t, (hbm, buf) in enumerate(((k_out, k_s), (v_out, v_s)))]

    cx = pltpu.make_async_copy(x_hbm, x_s, xw_sem.at[0])
    cw = pltpu.make_async_copy(w_hbm.at[layer], w_s, xw_sem.at[1])
    cx.start()
    cw.start()

    def start_loads(g, c):
        for cp in load(g):
            cp.start()
        return c

    cx.wait()
    cw.wait()
    lax.fori_loop(0, groups, start_loads, 0)
    if layer == 0:
        h = norm_rows(x_s[...].astype(F32), gain_ref[layer, 0:1, :], bias_ref[layer, 0:1, :])
    else:
        h = x_s[...]
    bq = bq_ref[layer].astype(F32)
    bq = jnp.concatenate([bq[t, j:j + 1] for t in range(3) for j in range(2)], axis=1)
    qkv = nt_dot(h, w_s[...]) + bq
    q_s[...] = qkv[:, :hd].astype(BF16)
    kvt = jnp.swapaxes(qkv[:, hd:], 0, 1).astype(BF16)
    for t in range(nb // 128):
        kvt_s[t] = kvt[:, t * 128:(t + 1) * 128]
    p_s[...] = jnp.zeros_like(p_s)

    row = lax.broadcasted_iota(jnp.int32, (GB, smax), 0)
    lane = lax.broadcasted_iota(jnp.int32, (GB, smax), 1)
    row_b = row.astype(F32).astype(BF16)
    lane_b = lane.astype(F32).astype(BF16)
    lane_h = lane // 64
    low_b = lane_b < 64
    zero = jnp.zeros((GB, hd), BF16)

    def weigh(g):
        o = nt_dot(p_s[...], v_s[rows(g)].reshape(GB * hd, smax))
        acc = jnp.zeros((GB, hd), F32)
        for i in range(GB):
            blk = o[:, i * hd:(i + 1) * hd]
            acc = jnp.where(row == i, jnp.where(lane_h == 0, blk[:GB], blk[GB:]), acc)
        a_ref[rows(g), :] = acc.astype(BF16)

    def group(g, carry):
        base = g * GB
        for cp in load(g):
            cp.wait()
        weigh(jnp.maximum(g - 1, 0))
        q16 = q_s[rows(g), :]
        lens = [len_ref[base + i] for i in range(GB)]
        lentile = jnp.zeros((GB, smax), jnp.int32)
        for i in range(GB):
            lentile = jnp.where(row == i, lens[i], lentile)
        tile = base // 128
        for i in range(GB):
            hit = lane_b == lens[i].astype(F32).astype(BF16)
            shift = lax.rem(lens[i] - (base + i) % 128 + 128, 128)
            for part, buf in ((0, k_s), (1, v_s)):
                cols = kvt_s[tile, part * hd:(part + 1) * hd, :]
                moved = pltpu.roll(cols, shift, 1)
                old = buf[base + i].reshape(hd // GB, GB, smax)
                buf[base + i] = jnp.where(hit[None], moved.reshape(hd // GB, GB, smax), old).reshape(2, 64, smax)
        for cp in save(g):
            cp.start()
        qh = [jnp.where(low_b, q16, zero), jnp.where(low_b, zero, q16)]
        qbd = jnp.concatenate(
            [jnp.concatenate([jnp.where(row_b == i, qh[h], zero) for i in range(GB)], axis=1) for h in range(2)], axis=0)
        s = jnp.dot(qbd, k_s[rows(g)].reshape(GB * hd, smax), preferred_element_type=F32) * 0.125
        seen = lane <= lentile
        s = jnp.where(jnp.concatenate([seen, seen], axis=0), s, -1e30)
        m = jnp.max(s, axis=-1, keepdims=True)
        ex = jnp.exp(s - m)
        p_s[...] = (ex / jnp.sum(ex, axis=-1, keepdims=True)).astype(BF16)
        return carry

    lax.fori_loop(0, groups, group, 0)
    weigh(groups - 1)

    def end_saves(g, c):
        for cp in save(g):
            cp.wait()
        return c

    lax.fori_loop(0, groups, end_saves, 0)


def attention(layer, cache_len, x, gain, bias, w_t, b_qkv, k_t, v_t, prev):
    nl, nb = k_t.shape[:2]
    vmem = pl.BlockSpec(memory_space=pltpu.VMEM)
    hbm = pl.BlockSpec(memory_space=pl.ANY)
    in_specs = [pl.BlockSpec(memory_space=pltpu.SMEM), vmem, vmem, vmem, hbm, hbm, hbm, hbm]
    operands = [cache_len, gain, bias, b_qkv, x, w_t, k_t, v_t]
    aliases = {}
    if prev is not None:
        in_specs += [hbm, hbm]
        operands += list(prev)
        aliases = {8: 0, 9: 1}
    groups = nb // GB
    return pl.pallas_call(
        functools.partial(attn_kernel, layer, prev is not None),
        in_specs=in_specs,
        out_specs=[hbm, hbm, vmem],
        out_shape=[jax.ShapeDtypeStruct(k_t.shape, BF16), jax.ShapeDtypeStruct(v_t.shape, BF16),
                   jax.ShapeDtypeStruct((nb, 128), BF16)],
        scratch_shapes=[
            pltpu.VMEM(x.shape, BF16), pltpu.VMEM(w_t.shape[1:], BF16),
            pltpu.VMEM(k_t.shape[1:], BF16), pltpu.VMEM(v_t.shape[1:], BF16),
            pltpu.VMEM((nb, 128), BF16), pltpu.VMEM((nb // 128, 256, 128), BF16), pltpu.VMEM((2 * GB, 128), BF16),
            pltpu.SemaphoreType.DMA((2, groups)), pltpu.SemaphoreType.DMA((2, groups)), pltpu.SemaphoreType.DMA((2,))],
        input_output_aliases=aliases,
        compiler_params=pltpu.CompilerParams(vmem_limit_bytes=63 * 2 ** 20),
        cost_estimate=pl.CostEstimate(flops=10 ** 9, bytes_accessed=2 ** 25, transcendentals=0),
        name=f"attention_{layer}",
    )(*operands)


def tail_kernel(layer, last, a_ref, x_in, gain_ref, bias_ref, bo_ref, bu_ref, bd_ref, wo_hbm, wu_hbm, wd_hbm, *rest):
    if last:
        out_ref, *rest = rest
        xrow_out = None
    else:
        out_ref, xrow_out, *rest = rest
    (wo, wu, wd, xs, hb, ob, act, own, dsend, drecv, csend, crecv, w_sem, x_sem,
     ds_sem, dr_sem, cs_sem, cr_sem, gs_sem, gr_sem) = rest
    nb, width = hb.shape
    me = lax.axis_index("tp")
    core = lax.rem(me, 2)
    chip = lax.div(me, 2)
    half = nb // 2
    cut = nb // 8
    far = (3, 1, 2)

    def chip_at(dist):
        xb, yb = lax.rem(chip, 2), lax.div(chip, 2)
        dx, dy = dist % 2, dist // 2
        nx = xb + dx - 2 * dx * xb
        ny = yb + dy - 2 * dy * yb
        return ny * 2 + nx

    sibling = chip * 2 + 1 - core
    peers = {d: chip_at(d) * 2 + core for d in far}

    loads = [pltpu.make_async_copy(h.at[layer], v, w_sem.at[i]) for i, (h, v) in enumerate(((wo_hbm, wo), (wu_hbm, wu), (wd_hbm, wd)))]
    for cp in loads:
        cp.start()
    row0 = pl.multiple_of((core * 4 + chip) * cut, cut)
    if layer == 0:
        cx = pltpu.make_async_copy(x_in.at[pl.ds(row0, cut)], xs, x_sem)
        cx.start()

    barrier = pltpu.get_barrier_semaphore()
    for dev in [sibling] + [peers[d] for d in far]:
        pl.semaphore_signal(barrier, inc=1, device_id={"tp": dev}, device_id_type=MESH)
    pl.semaphore_wait(barrier, 4)

    def block(ref, c, k):
        return ref.at[pl.ds(pl.multiple_of((k * 4 + c) * cut, cut), cut)]

    def scatter(r, act_ref, w_ref):
        other = pl.multiple_of((1 - core) * half, half)
        dsend[r] = jnp.dot(act_ref[pl.ds(other, half), :], w_ref[...], preferred_element_type=F32).astype(BF16)
        d2d = {}
        for n, d in enumerate(far + (0,)):
            cs = pl.ds(pl.multiple_of(chip_at(d) * cut, cut), cut)
            d2d[d] = pltpu.make_async_remote_copy(dsend.at[r, cs], drecv.at[r, cs], ds_sem.at[r, n], dr_sem.at[r, n],
                                                  device_id={"tp": sibling}, device_id_type=MESH)
            d2d[d].start()
        own[...] = jnp.dot(act_ref[pl.ds(pl.multiple_of(core * half, half), half), :], w_ref[...], preferred_element_type=F32)
        sends = []
        for n, d in enumerate(far):
            cs = pl.ds(pl.multiple_of(chip_at(d) * cut, cut), cut)
            d2d[d].wait_recv()
            csend[r, n] = (own[cs, :] + drecv[r, cs, :].astype(F32)).astype(BF16)
            cp = pltpu.make_async_remote_copy(csend.at[r, n], crecv.at[r, n], cs_sem.at[r, n], cr_sem.at[r, n],
                                              device_id={"tp": peers[d]}, device_id_type=MESH)
            cp.start()
            sends.append(cp)
        cs = pl.ds(pl.multiple_of(chip * cut, cut), cut)
        d2d[0].wait_recv()
        total = own[cs, :] + drecv[r, cs, :].astype(F32)
        for n in (1, 2, 0):
            sends[n].wait_recv()
            total = total + crecv[r, n].astype(F32)
        return total, [*d2d.values(), *sends]

    def gather(r, buf, rows):
        block(buf, chip, core)[...] = rows
        mine = block(buf, chip, core)
        first = {}
        for n, (d, dev) in enumerate([(d, peers[d]) for d in far] + [(0, sibling)]):
            first[d] = pltpu.make_async_remote_copy(mine, mine, gs_sem.at[r, n], gr_sem.at[r, n],
                                                    device_id={"tp": dev}, device_id_type=MESH)
            first[d].start()
        second = []
        for n, d in ((1, 1), (2, 2), (0, 3)):
            c = chip_at(d)
            pltpu.make_async_remote_copy(mine, block(buf, c, core), gs_sem.at[r, n], gr_sem.at[r, n],
                                         device_id={"tp": peers[d]}, device_id_type=MESH).wait_recv()
            cp = pltpu.make_async_remote_copy(block(buf, c, core), block(buf, c, core), gs_sem.at[r, 4 + n], gr_sem.at[r, 4 + n],
                                              device_id={"tp": sibling}, device_id_type=MESH)
            cp.start()
            second.append(cp)
        first[0].wait_recv()
        for cp in second:
            cp.wait_recv()
        return [*first.values(), *second]

    loads[0].wait()
    total, pending = scatter(0, a_ref, wo)
    if layer == 0:
        cx.wait()
        xrow = xs[...]
    else:
        xrow = x_in[...]
    xmid = (xrow.astype(F32) + total + bo_ref[...].astype(F32)[layer:layer + 1]).astype(BF16)
    pending += gather(0, hb, norm_rows(xmid.astype(F32), gain_ref[layer, 1:2, :], bias_ref[layer, 1:2, :]))
    loads[1].wait()
    up = jnp.dot(hb[...], wu[...], preferred_element_type=F32) + bu_ref[...].astype(F32)[layer:layer + 1]
    act[...] = jnp.maximum(up, 0.0).astype(BF16)
    loads[2].wait()
    total, started = scatter(1, act, wd)
    pending += started
    xnew = (xmid.astype(F32) + total + bd_ref[...].astype(F32)[layer:layer + 1]).astype(BF16)
    if last:
        rows = xnew
    else:
        xrow_out[...] = xnew
        rows = norm_rows(xnew.astype(F32), gain_ref[layer + 1, 0:1, :], bias_ref[layer + 1, 0:1, :])
    pending += gather(1, ob, rows)
    out_ref[...] = ob[...]
    for cp in pending:
        cp.wait_send()


def tail(layer, last, a, x, gain, bias, b_out, b_up, b_down, w_out, w_up, w_down):
    nb = a.shape[0]
    width = w_out.shape[-1]
    hidden = w_up.shape[-1]
    cut = nb // 8
    vmem = pl.BlockSpec(memory_space=pltpu.VMEM)
    hbm = pl.BlockSpec(memory_space=pl.ANY)
    out_shape = [jax.ShapeDtypeStruct((nb, width), BF16)]
    if not last:
        out_shape.append(jax.ShapeDtypeStruct((cut, width), BF16))
    return pl.pallas_call(
        functools.partial(tail_kernel, layer, last),
        in_specs=[vmem, hbm if layer == 0 else vmem, vmem, vmem, vmem, vmem, vmem, hbm, hbm, hbm],
        out_specs=[vmem] * len(out_shape),
        out_shape=out_shape,
        scratch_shapes=[
            pltpu.VMEM(w_out.shape[1:], BF16), pltpu.VMEM(w_up.shape[1:], BF16), pltpu.VMEM(w_down.shape[1:], BF16),
            pltpu.VMEM((cut, width), BF16), pltpu.VMEM((nb, width), BF16), pltpu.VMEM((nb, width), BF16),
            pltpu.VMEM((nb, hidden), BF16), pltpu.VMEM((nb // 2, width), F32),
            pltpu.VMEM((2, nb // 2, width), BF16), pltpu.VMEM((2, nb // 2, width), BF16),
            pltpu.VMEM((2, 3, cut, width), BF16), pltpu.VMEM((2, 3, cut, width), BF16),
            pltpu.SemaphoreType.DMA((3,)), pltpu.SemaphoreType.DMA,
            pltpu.SemaphoreType.DMA((2, 4)), pltpu.SemaphoreType.DMA((2, 4)),
            pltpu.SemaphoreType.DMA((2, 3)), pltpu.SemaphoreType.DMA((2, 3)),
            pltpu.SemaphoreType.DMA((2, 7)), pltpu.SemaphoreType.DMA((2, 7))],
        compiler_params=pltpu.CompilerParams(collective_id=layer, has_side_effects=True, vmem_limit_bytes=63 * 2 ** 20),
        cost_estimate=pl.CostEstimate(flops=10 ** 9, bytes_accessed=2 ** 22, transcendentals=0),
        name=f"tail_{layer}",
    )(a, x, gain, bias, b_out, b_up, b_down, w_out, w_up, w_down)


def solution(mesh):
    cache_spec = P(None, 'dp', 'tp', None, None)
    in_specs = (P('dp', None), P('dp'), cache_spec, cache_spec, P(), P(),
                P(None, None, None, 'tp', None), P(None, None, 'tp', None),
                P(None, 'tp', None, None), P(), P(None, None, 'tp'), P(None, 'tp'),
                P(None, 'tp', None), P())
    out_specs = (P('dp', None), cache_spec, cache_spec)

    def local_step(x, cache_len, k_cache, v_cache, norm_gain, norm_bias, w_qkv, b_qkv, w_out, b_out, w_up, b_up, w_down, b_down):
        layers = k_cache.shape[0]
        width = x.shape[1]
        k_t, v_t = k_cache.swapaxes(3, 4), v_cache.swapaxes(3, 4)
        w_t = w_qkv.transpose(0, 2, 3, 4, 1).reshape(layers, -1, width)
        w_o = w_out.reshape(layers, -1, width)
        h, xrow, caches = x, x, None
        for layer in range(layers):
            last = layer == layers - 1
            *caches, att = attention(layer, cache_len, h, norm_gain, norm_bias, w_t, b_qkv, k_t, v_t, caches)
            outs = tail(layer, last, att, xrow, norm_gain, norm_bias, b_out, b_up, b_down, w_o, w_up, w_down)
            h = outs[0]
            if not last:
                xrow = outs[1]
        return h, caches[0].swapaxes(3, 4), caches[1].swapaxes(3, 4)

    return jax.shard_map(local_step, mesh=mesh, in_specs=in_specs, out_specs=out_specs, check_vma=False)
```

time: 263 us -> 90.9 us (0.35)
  waiting for transfers between devices: 142 us -> 0 us
  Pallas kernels: 0 us -> 87.7 us
  other arithmetic: 57.2 us -> 0 us
  matrix products: 42.4 us -> 0 us
  between operations: 14 us -> 0.66 us
    psum x4 -> x0, waiting for transfers between devices: 142 us -> none  [the longest x2 71.7 us: local_step(): attn_sum = lax.psum(attn_part, 'tp')]
    pallas_call x0 -> x4, Pallas kernels: none -> 87.7 us  [the longest x2 57.3 us: tail(): pl.pallas_call(functools.partial(tail_kernel, layer, last), in_specs=[vme...]
    dot_general x8 -> x0, matrix products: 40.3 us -> none  [the longest x2 15.9 us: local_step(): jnp.einsum('bhj,bhjd->bhd', attn_prob, v_layer, preferred_element_type=jn...]
    another operation x1 -> x0, other arithmetic: 22.8 us -> none  [local_step(): return (x, jnp.stack(k_layers), jnp.stack(v_layers))]
    select_n x1 -> x0, other arithmetic: 22.8 us -> none  [local_step(): v_layer = jnp.where(write_here, qkv_all[:, 2, :, None, :], v_cache[layer])]
    reduce_sum x8 -> x0, other arithmetic: 7.28 us -> none  [the longest x4 5.11 us: layer_norm(): row_mean = jnp.mean(vec_f, axis=-1, keepdims=True)]
    slice x3 -> x0, local copies, waits for them, and re-layouts: 3.13 us -> none  [the longest x2 1.58 us: local_step(): hidden_mlp = layer_norm(x_mid, norm_gain[layer, 1], norm_bias[layer, 1])]
  transfers between devices with their start and end apart: 4 -> 0, of which waited for: 4 -> 0; matrix products, arithmetic and copies ran while one was open for 18% -> 0% of each run, Pallas kernels for 0% -> 0%
where the time goes in v1:
time: 90.9 us; the launch traced here: 90.2 us
  Pallas kernels  87.7 us (96%)
  local copies, waits for them, and re-layouts  1.87 us (2%)
    pallas_call x2, Pallas kernels, tail(): pl.pallas_call(functools.partial(tail_kernel, layer, last), in_specs=[vme...  57.3 us
    pallas_call x2, Pallas kernels, attention(): pl.pallas_call(functools.partial(attn_kernel, layer, prev is not None), i...  30.3 us
    unnamed x1, local copies, waits for them, and re-layouts  1.87 us

profile of v1, /device:TPU:1, one launch (start us, length us, event | category | flops | bytes accessed | tf_op | source)
XLA Modules:
  0.0 90.2 jit_solution(7945320987887515222)
XLA Ops:
  0.6 15.2 %attention_0.1 = (bf16[2,256,2,64,128]{4,3,2,1,0:T(8,128)(2,1)}, bf16[2,256,2,64,128]{4,3,2,1,0:T(8,128)(2,1)}, bf16[256,128]{1,0:T(8,128)(2,1)}) custom-call(s32[256]{0:T(256)} %len_ref.3, f32[2,2,1024]{2,1,0:T(2,128)} %gain_ref.7, f32[2,2,1024]{2,1,0:T(2,128)} %bias_ref.7, bf16[2,3,2,64]{3,2,1,0:T(2,128)(2,1)} %bq_ref.3, bf16[256,1024]{1,0:T(8,128)(2,1)} %x_in.1, ...), custom_call_target="tpu_custom_call" | custom-call | flops 1000000000 | bytes 33554432 | tf_op jit(solution)/shard_map/attention_0/pallas_call | solution.py:145
  15.8 29.8 %tail_0.1 = (bf16[256,1024]{1,0:T(8,128)(2,1)}, bf16[32,1024]{1,0:T(8,128)(2,1)}) custom-call(bf16[256,128]{1,0:T(8,128)(2,1)} %get-tuple-element.11.a_ref, bf16[256,1024]{1,0:T(8,128)(2,1)} %x_in.1, f32[2,2,1024]{2,1,0:T(2,128)} %gain_ref.7, f32[2,2,1024]{2,1,0:T(2,128)} %bias_ref.7, bf16[2,1024]{1,0:T(2,128)(2,1)} %bo_ref.3, bf16[2,512]{1,0:T(2,128)(2,1)} %bu_ref.3, ...), custom_call_target="tpu_custom_call" | custom-call | flops 1000000000 | bytes 4194304 | tf_op jit(solution)/shard_map/tail_0/pallas_call | solution.py:291
  45.6 15.2 %attention_1.1 = (bf16[2,256,2,64,128]{4,3,2,1,0:T(8,128)(2,1)}, bf16[2,256,2,64,128]{4,3,2,1,0:T(8,128)(2,1)}, bf16[256,128]{1,0:T(8,128)(2,1)}) custom-call(s32[256]{0:T(256)} %len_ref.3, f32[2,2,1024]{2,1,0:T(2,128)} %gain_ref.7, f32[2,2,1024]{2,1,0:T(2,128)} %bias_ref.7, ...), custom_call_target="tpu_custom_call", output_to_operand_aliasing={{0}: (8, {}), {1}: (9, {})} | custom-call | flops 1000000000 | bytes 33554432 | tf_op jit(solution)/shard_map/attention_1/pallas_call | solution.py:145
  60.8 27.6 %tail_1.1 = bf16[256,1024]{1,0:T(8,128)(2,1)} custom-call(bf16[256,128]{1,0:T(8,128)(2,1)} %get-tuple-element.15.a_ref, bf16[32,1024]{1,0:T(8,128)(2,1)} %get-tuple-element.16.x_in, f32[2,2,1024]{2,1,0:T(2,128)} %gain_ref.7, f32[2,2,1024]{2,1,0:T(2,128)} %bias_ref.7, bf16[2,1024]{1,0:T(2,128)(2,1)} %bo_ref.3, bf16[2,512]{1,0:T(2,128)(2,1)} %bu_ref.3, ...), custom_call_target="tpu_custom_call" | custom-call | flops 1000000000 | bytes 4194304 | tf_op jit(solution)/shard_map/tail_1/pallas_call | solution.py:291
  88.3 1.9 %copy.22 = bf16[256,1024]{1,0:T(8,128)(2,1)} copy(bf16[256,1024]{1,0:T(8,128)(2,1)} %tail_1.1) | data formatting | bytes 1048576

commit v2 on v0

v2 whole, which is shorter than its diff:
```python
import functools

import jax
import jax.numpy as jnp
from jax import lax
from jax.experimental import pallas as pl
from jax.experimental.pallas import tpu as pltpu
from jax.sharding import PartitionSpec as P

F32 = jnp.float32
BF16 = jnp.bfloat16
EPS = 1e-5
MESH = pl.DeviceIdType.MESH
GB = 32
ATTN_VMEM = 63 * 2 ** 20
EARLY = 4


def norm_rows(xf, gain, bias):
    mean = jnp.mean(xf, axis=-1, keepdims=True)
    cen = xf - mean
    var = jnp.mean(cen * cen, axis=-1, keepdims=True)
    return (cen * lax.rsqrt(var + EPS) * gain + bias).astype(BF16)


def nt_dot(a, b):
    return lax.dot_general(a, b, (((1,), (1,)), ((), ())), preferred_element_type=F32)


def attn_kernel(layer, aliased, len_hbm, gain_hbm, bias_hbm, bq_hbm, x_in, w_hbm, k_hbm, v_hbm, *rest):
    if aliased:
        rest = rest[2:]
    k_out, v_out, a_out, len_ref, gain_ref, bias_ref, bq_ref, h_s, w_s, k_s, v_s, q_s, kvt_s, a_ref, in_sem, out_sem, a_sem, first_sem = rest
    nb = h_s.shape[0]
    hd = 128
    smax = 128
    groups = nb // GB

    def rows(g):
        return pl.ds(g * GB, GB)

    def load(g):
        return [pltpu.make_async_copy(hbm.at[layer, rows(g)], buf.at[rows(g)], in_sem.at[t, g])
                for t, (hbm, buf) in enumerate(((k_hbm, k_s), (v_hbm, v_s)))]

    def save_a(g):
        return pltpu.make_async_copy(a_ref.at[rows(g)], a_out.at[rows(g)], a_sem.at[g])

    def save(g):
        return [pltpu.make_async_copy(buf.at[rows(g)], hbm.at[layer, rows(g)], out_sem.at[t, g])
                for t, (hbm, buf) in enumerate(((k_out, k_s), (v_out, v_s)))]

    pairs = [(x_in, h_s), (w_hbm.at[layer], w_s), (bq_hbm, bq_ref), (len_hbm, len_ref)]
    if layer == 0:
        pairs += [(gain_hbm, gain_ref), (bias_hbm, bias_ref)]
    first = [pltpu.make_async_copy(src, dst, first_sem.at[i]) for i, (src, dst) in enumerate(pairs)]
    for cp in first:
        cp.start()
    for g in range(EARLY):
        for cp in load(g):
            cp.start()
    for cp in first:
        cp.wait()
    for g in range(EARLY, groups):
        for cp in load(g):
            cp.start()
    if layer == 0:
        for r in range(0, nb, 64):
            h_s[r:r + 64] = norm_rows(h_s[r:r + 64].astype(F32), gain_ref[layer, 0:1, :], bias_ref[layer, 0:1, :])
    bq = bq_ref[layer].astype(F32)
    bq = jnp.concatenate([bq[t, j:j + 1] for t in range(3) for j in range(2)], axis=1)
    qkv = nt_dot(h_s[...], w_s[...]) + bq
    q_s[...] = qkv[:, :hd].astype(BF16)
    kvt = jnp.swapaxes(qkv[:, hd:], 0, 1).astype(BF16)
    for t in range(nb // 128):
        kvt_s[t] = kvt[:, t * 128:(t + 1) * 128]

    row = lax.broadcasted_iota(jnp.int32, (GB, smax), 0)
    lane = lax.broadcasted_iota(jnp.int32, (GB, smax), 1)
    row_b = row.astype(F32).astype(BF16)
    lane_b = lane.astype(F32).astype(BF16)
    lane_c = lane_b[:16]
    lane_h = lane // 64
    low_b = lane_b < 64
    zero = jnp.zeros((GB, hd), BF16)
    even2 = lax.rem(lax.broadcasted_iota(jnp.int32, (2 * GB, smax), 0), 2).astype(F32).astype(BF16) < 0.5
    pair_of = lax.rem(lax.broadcasted_iota(jnp.int32, (hd, 2 * GB), 1), GB) // 2

    def weigh(g, p):
        nil = jnp.zeros_like(p)
        weights = jnp.concatenate([jnp.where(even2, p, nil), jnp.where(even2, nil, p)], axis=1)
        v = v_s[rows(g)].reshape(GB // 2, 2, hd, smax)
        pairs = jnp.concatenate([v[:, 0], v[:, 1]], axis=2).reshape(GB // 2 * hd, 2 * smax)
        o = nt_dot(pairs, weights)
        acc = o[:hd]
        for i in range(1, GB // 2):
            acc = jnp.where(pair_of == i, o[i * hd:(i + 1) * hd], acc)
        acc = jnp.swapaxes(acc, 0, 1)
        a_ref[rows(g), :] = jnp.where(lane_h == 0, acc[:GB], acc[GB:]).astype(BF16)
        save_a(g).start()

    def probs(g, lens):
        q = q_s[rows(g), :]
        qh = [jnp.where(low_b, q, zero), jnp.where(low_b, zero, q)]
        qbd = jnp.concatenate(
            [jnp.concatenate([jnp.where(row_b == i, qh[h], zero) for i in range(GB)], axis=1) for h in range(2)], axis=0)
        s = jnp.dot(qbd, k_s[rows(g)].reshape(GB * hd, smax), preferred_element_type=F32) * 0.125
        lentile = jnp.zeros((GB, smax), jnp.int32)
        for i in range(GB):
            lentile = jnp.where(row == i, lens[i], lentile)
        seen = lane <= lentile
        s = jnp.where(jnp.concatenate([seen, seen], axis=0), s, -1e30)
        m = jnp.max(s, axis=-1, keepdims=True)
        ex = jnp.exp(s - m)
        return (ex / jnp.sum(ex, axis=-1, keepdims=True)).astype(BF16)

    def insert(g, lens):
        for i in range(GB):
            b = g * GB + i
            hit = lane_c == lens[i].astype(F32).astype(BF16)
            shift = lax.rem(lens[i] - b % 128 + 128, 128)
            for part, buf in ((0, k_s), (1, v_s)):
                moved = pltpu.roll(kvt_s[b // 128, part * hd:(part + 1) * hd, :], shift, 1)
                old = buf[b].reshape(hd // 16, 16, smax)
                buf[b] = jnp.where(hit[None], moved.reshape(hd // 16, 16, smax), old).reshape(2, 64, smax)

    lens, p = {}, {}
    for g in range(groups + 2):
        if g < groups:
            for cp in load(g):
                cp.wait()
            lens[g] = [len_ref[g * GB + i] for i in range(GB)]
        if g >= 2:
            weigh(g - 2, p.pop(g - 2))
        if 1 <= g <= groups:
            p[g - 1] = probs(g - 1, lens[g - 1])
        if g < groups:
            insert(g, lens[g])
            for cp in save(g):
                cp.start()
    for g in range(groups):
        for cp in save(g) + [save_a(g)]:
            cp.wait()


def attention(layer, cache_len, x, gain, bias, w_t, b_qkv, k_t, v_t, prev):
    nl, nb = k_t.shape[:2]
    hbm = pl.BlockSpec(memory_space=pltpu.HBM)
    in_specs = [hbm, hbm, hbm, hbm, hbm, hbm, hbm, hbm]
    operands = [cache_len, gain, bias, b_qkv, x, w_t, k_t, v_t]
    aliases = {}
    if prev is not None:
        in_specs += [hbm, hbm]
        operands += list(prev)
        aliases = {8: 0, 9: 1}
    groups = nb // GB
    return pl.pallas_call(
        functools.partial(attn_kernel, layer, prev is not None),
        in_specs=in_specs,
        out_specs=[hbm, hbm, hbm],
        out_shape=[jax.ShapeDtypeStruct(k_t.shape, BF16), jax.ShapeDtypeStruct(v_t.shape, BF16),
                   jax.ShapeDtypeStruct((nb, 128), BF16)],
        scratch_shapes=[
            pltpu.SMEM(cache_len.shape, jnp.int32), pltpu.VMEM(gain.shape, F32), pltpu.VMEM(bias.shape, F32), pltpu.VMEM(b_qkv.shape, BF16),
            pltpu.VMEM(x.shape, BF16), pltpu.VMEM(w_t.shape[1:], BF16),
            pltpu.VMEM(k_t.shape[1:], BF16), pltpu.VMEM(v_t.shape[1:], BF16),
            pltpu.VMEM((nb, 128), BF16), pltpu.VMEM((nb // 128, 256, 128), BF16), pltpu.VMEM((nb, 128), BF16),
            pltpu.SemaphoreType.DMA((2, groups)), pltpu.SemaphoreType.DMA((2, groups)), pltpu.SemaphoreType.DMA((groups,)), pltpu.SemaphoreType.DMA((6,))],
        input_output_aliases=aliases,
        compiler_params=pltpu.CompilerParams(vmem_limit_bytes=ATTN_VMEM),
        cost_estimate=pl.CostEstimate(flops=10 ** 9, bytes_accessed=2 ** 25, transcendentals=0),
        name=f"attention_{layer}",
    )(*operands)


def tail_kernel(layer, last, a_hbm, x_hbm, gain_hbm, bias_hbm, bo_hbm, bu_hbm, bd_hbm, wo_hbm, wu_hbm, wd_hbm, *rest):
    if last:
        out_hbm, *rest = rest
    else:
        out_hbm, xrow_out, *rest = rest
    (a_s, gain_ref, bias_ref, bo_ref, bu, bd_ref, wo, wu, wd, xs, bu_x, wu_x, wd_x, hb, ob, own, dsend, drecv, csend, crecv,
     w_sem, o_sem, xs_sem, xr_sem, ds_sem, dr_sem, cs_sem, cr_sem, hs_sem, hr_sem, gs_sem, gr_sem) = rest
    nb = ob.shape[0]
    me = lax.axis_index("tp")
    core = lax.rem(me, 2)
    chip = lax.div(me, 2)
    half = nb // 2
    cut = nb // 8
    far = (3, 1, 2)

    def chip_at(dist):
        xb, yb = lax.rem(chip, 2), lax.div(chip, 2)
        dx, dy = dist % 2, dist // 2
        return (yb + dy - 2 * dy * yb) * 2 + xb + dx - 2 * dx * xb

    sibling = chip * 2 + 1 - core
    peers = {d: chip_at(d) * 2 + core for d in far}

    def send(src, dst, s_sem, r_sem, dev):
        return pltpu.make_async_remote_copy(src, dst, s_sem, r_sem, device_id={"tp": dev}, device_id_type=MESH)

    def slot(d):
        return pl.ds(pl.multiple_of(chip_at(d) * cut, cut), cut)

    row0 = pl.multiple_of(core * half + chip * cut, cut)
    x_mine = x_hbm.at[pl.ds(row0, cut)] if layer == 0 else x_hbm
    pairs = [(a_hbm, a_s), (wo_hbm.at[layer], wo), (x_mine, xs), (gain_hbm, gain_ref), (bias_hbm, bias_ref), (bo_hbm, bo_ref),
             (bu_hbm, bu), (bd_hbm, bd_ref), (wu_hbm.at[layer], wu), (wd_hbm.at[layer], wd)]
    loads = [pltpu.make_async_copy(src, dst, w_sem.at[i]) for i, (src, dst) in enumerate(pairs)]
    for cp in loads:
        cp.start()
    barrier = pltpu.get_barrier_semaphore()
    for dev in [sibling] + [peers[d] for d in far]:
        pl.semaphore_signal(barrier, inc=1, device_id={"tp": dev}, device_id_type=MESH)

    for cp in loads[:2]:
        cp.wait()
    dsend[...] = jnp.dot(a_s[pl.ds(pl.multiple_of((1 - core) * half, half), half), :], wo[...], preferred_element_type=F32).astype(BF16)
    pl.semaphore_wait(barrier, 4)
    d2d = {d: send(dsend.at[slot(d)], drecv.at[slot(d)], ds_sem.at[n], dr_sem.at[n], sibling) for n, d in enumerate(far + (0,))}
    for d in far + (0,):
        d2d[d].start()
    swap = [send(src, dst, xs_sem.at[n], xr_sem.at[n], sibling)
            for n, (src, dst) in enumerate(((bu_hbm, bu_x), (wu_hbm.at[layer], wu_x), (wd_hbm.at[layer], wd_x)))]
    for cp in swap:
        cp.start()
    own[...] = jnp.dot(a_s[pl.ds(pl.multiple_of(core * half, half), half), :], wo[...], preferred_element_type=F32)
    sends = {}
    for n, d in enumerate(far):
        d2d[d].wait_recv()
        csend[0, n] = (own[slot(d), :] + drecv[slot(d), :].astype(F32)).astype(BF16)
        sends[0, d] = send(csend.at[0, n], crecv.at[0, n], cs_sem.at[0, n], cr_sem.at[0, n], peers[d])
        sends[0, d].start()
    d2d[0].wait_recv()
    total = own[slot(0), :] + drecv[slot(0), :].astype(F32)
    for cp in loads[2:]:
        cp.wait()
    for n, d in ((2, 2), (1, 1), (0, 3)):
        sends[0, d].wait_recv()
        total = total + crecv[0, n].astype(F32)
    xmid = (xs[...].astype(F32) + total + bo_ref[...].astype(F32)[layer:layer + 1]).astype(BF16)

    hb[slot(0), :] = norm_rows(xmid.astype(F32), gain_ref[layer, 1:2, :], bias_ref[layer, 1:2, :])
    hsend = {d: send(hb.at[slot(0)], hb.at[slot(0)], hs_sem.at[n], hr_sem.at[n], peers[d]) for n, d in enumerate(far)}
    for d in far:
        hsend[d].start()
    for cp in swap:
        cp.wait_recv()

    def mlp(h):
        part = None
        for b_ref, u_ref, w_ref in ((bu, wu, wd), (bu_x, wu_x, wd_x)):
            up = jnp.dot(h, u_ref[...], preferred_element_type=F32) + b_ref[...].astype(F32)[layer:layer + 1]
            y = jnp.dot(jnp.maximum(up, 0.0).astype(BF16), w_ref[...], preferred_element_type=F32)
            part = y if part is None else part + y
        return part

    def arrived(d):
        n = far.index(d)
        send(hb.at[slot(0)], hb.at[slot(d)], hs_sem.at[n], hr_sem.at[n], peers[d]).wait_recv()

    total = mlp(hb[slot(0), :])
    for together in ((2, 3), (1,)):
        for d in together:
            arrived(d)
        part = mlp(jnp.concatenate([hb[slot(d), :] for d in together], axis=0))
        for i, d in sorted(enumerate(together), key=lambda t: -t[1]):
            n = far.index(d)
            csend[1, n] = part[i * cut:(i + 1) * cut].astype(BF16)
            sends[1, d] = send(csend.at[1, n], crecv.at[1, n], cs_sem.at[1, n], cr_sem.at[1, n], peers[d])
            sends[1, d].start()
    for n, d in ((2, 2), (0, 3), (1, 1)):
        sends[1, d].wait_recv()
        total = total + crecv[1, n].astype(F32)
    xnew = (xmid.astype(F32) + total + bd_ref[...].astype(F32)[layer:layer + 1]).astype(BF16)

    def block(d, k):
        return ob.at[pl.ds(pl.multiple_of(k * half + chip_at(d) * cut, cut), cut)]

    def keep(d, k, n):
        cp = pltpu.make_async_copy(block(d, k), out_hbm.at[pl.ds(pl.multiple_of(k * half + chip_at(d) * cut, cut), cut)], o_sem.at[n])
        cp.start()
        return cp

    mine = block(0, core)
    if last:
        mine[...] = xnew
    else:
        mine[...] = norm_rows(xnew.astype(F32), gain_ref[layer + 1, 0:1, :], bias_ref[layer + 1, 0:1, :])
    spread = {d: send(mine, mine, gs_sem.at[n], gr_sem.at[n], dev) for n, (d, dev) in enumerate([(d, peers[d]) for d in far] + [(0, sibling)])}
    for d in far + (0,):
        spread[d].start()
    kept = [keep(0, core, 0)]
    if not last:
        xs[...] = xnew
        kept.append(pltpu.make_async_copy(xs, xrow_out, o_sem.at[8]))
        kept[-1].start()
    passed = {}
    for d in (2, 3, 1):
        n = far.index(d)
        send(mine, block(d, core), gs_sem.at[n], gr_sem.at[n], peers[d]).wait_recv()
        passed[d] = send(block(d, core), block(d, core), gs_sem.at[4 + n], gr_sem.at[4 + n], sibling)
        passed[d].start()
        kept.append(keep(d, core, 1 + n))
    spread[0].wait_recv()
    kept.append(keep(0, 1 - core, 4))
    for d in (2, 3, 1):
        passed[d].wait_recv()
        kept.append(keep(d, 1 - core, 5 + far.index(d)))
    for cp in [*d2d.values(), *swap, *sends.values(), *hsend.values(), *spread.values(), *passed.values()]:
        cp.wait_send()
    for cp in kept:
        cp.wait()


def tail(layer, last, a, x, gain, bias, b_out, b_up, b_down, w_out, w_up, w_down):
    nb = a.shape[0]
    width = w_out.shape[-1]
    half, cut = nb // 2, nb // 8
    hbm = pl.BlockSpec(memory_space=pltpu.HBM)
    out_shape = [jax.ShapeDtypeStruct((nb, width), BF16)]
    if not last:
        out_shape.append(jax.ShapeDtypeStruct((cut, width), BF16))
    dma = pltpu.SemaphoreType.DMA
    return pl.pallas_call(
        functools.partial(tail_kernel, layer, last),
        in_specs=[hbm] * 10,
        out_specs=[hbm] * len(out_shape),
        out_shape=out_shape,
        scratch_shapes=[
            pltpu.VMEM(a.shape, BF16), pltpu.VMEM(gain.shape, F32), pltpu.VMEM(bias.shape, F32),
            pltpu.VMEM(b_out.shape, BF16), pltpu.VMEM(b_up.shape, BF16), pltpu.VMEM(b_down.shape, BF16),
            pltpu.VMEM(w_out.shape[1:], BF16), pltpu.VMEM(w_up.shape[1:], BF16), pltpu.VMEM(w_down.shape[1:], BF16),
            pltpu.VMEM((cut, width), BF16),
            pltpu.VMEM(b_up.shape, BF16), pltpu.VMEM(w_up.shape[1:], BF16), pltpu.VMEM(w_down.shape[1:], BF16),
            pltpu.VMEM((half, width), BF16), pltpu.VMEM((nb, width), BF16), pltpu.VMEM((half, width), F32),
            pltpu.VMEM((half, width), BF16), pltpu.VMEM((half, width), BF16),
            pltpu.VMEM((2, 3, cut, width), BF16), pltpu.VMEM((2, 3, cut, width), BF16),
            dma((10,)), dma((9,)), dma((3,)), dma((3,)), dma((4,)), dma((4,)),
            dma((2, 3)), dma((2, 3)), dma((3,)), dma((3,)), dma((7,)), dma((7,))],
        compiler_params=pltpu.CompilerParams(collective_id=layer, has_side_effects=True, vmem_limit_bytes=ATTN_VMEM),
        cost_estimate=pl.CostEstimate(flops=10 ** 9, bytes_accessed=2 ** 22, transcendentals=0),
        name=f"tail_{layer}",
    )(a, x, gain, bias, b_out, b_up, b_down, w_out, w_up, w_down)


def solution(mesh):
    cache_spec = P(None, 'dp', 'tp', None, None)
    in_specs = (P('dp', None), P('dp'), cache_spec, cache_spec, P(), P(),
                P(None, None, None, 'tp', None), P(None, None, 'tp', None),
                P(None, 'tp', None, None), P(), P(None, None, 'tp'), P(None, 'tp'),
                P(None, 'tp', None), P())
    out_specs = (P('dp', None), cache_spec, cache_spec)

    def local_step(x, cache_len, k_cache, v_cache, norm_gain, norm_bias, w_qkv, b_qkv, w_out, b_out, w_up, b_up, w_down, b_down):
        layers = k_cache.shape[0]
        width = x.shape[1]
        k_t, v_t = k_cache.swapaxes(3, 4), v_cache.swapaxes(3, 4)
        w_t = w_qkv.transpose(0, 2, 3, 4, 1).reshape(layers, -1, width)
        w_o = w_out.reshape(layers, -1, width)
        h, xrow, caches = x, x, None
        for layer in range(layers):
            last = layer == layers - 1
            *caches, att = attention(layer, cache_len, h, norm_gain, norm_bias, w_t, b_qkv, k_t, v_t, caches)
            outs = tail(layer, last, att, xrow, norm_gain, norm_bias, b_out, b_up, b_down, w_o, w_up, w_down)
            h = outs[0]
            if not last:
                xrow = outs[1]
        return h, caches[0].swapaxes(3, 4), caches[1].swapaxes(3, 4)

    return jax.shard_map(local_step, mesh=mesh, in_specs=in_specs, out_specs=out_specs, check_vma=False)
```

time: 263 us -> 79.1 us (0.30); the launches traced: 260 us -> 78.9 us
  waiting for transfers between devices: 142 us -> 0 us
  Pallas kernels: 0 us -> 76.4 us
  other arithmetic: 57.2 us -> 0 us
  matrix products: 42.4 us -> 0 us
  between operations: 14 us -> 0.66 us
    psum x4 -> x0, waiting for transfers between devices: 142 us -> none  [the longest x2 71.7 us: local_step(): attn_sum = lax.psum(attn_part, 'tp')]
    pallas_call x0 -> x4, Pallas kernels: none -> 76.4 us  [the longest x2 50.6 us: tail(): pl.pallas_call(functools.partial(tail_kernel, layer, last), in_specs=[hbm...]
    dot_general x8 -> x0, matrix products: 40.3 us -> none  [the longest x2 15.9 us: local_step(): jnp.einsum('bhj,bhjd->bhd', attn_prob, v_layer, preferred_element_type=jn...]
    another operation x1 -> x0, other arithmetic: 22.8 us -> none  [local_step(): return (x, jnp.stack(k_layers), jnp.stack(v_layers))]
    select_n x1 -> x0, other arithmetic: 22.8 us -> none  [local_step(): v_layer = jnp.where(write_here, qkv_all[:, 2, :, None, :], v_cache[layer])]
    reduce_sum x8 -> x0, other arithmetic: 7.28 us -> none  [the longest x4 5.11 us: layer_norm(): row_mean = jnp.mean(vec_f, axis=-1, keepdims=True)]
    slice x3 -> x0, local copies, waits for them, and re-layouts: 3.13 us -> none  [the longest x2 1.58 us: local_step(): hidden_mlp = layer_norm(x_mid, norm_gain[layer, 1], norm_bias[layer, 1])]
  transfers between devices with their start and end apart: 4 -> 0, of which waited for: 4 -> 0; matrix products, arithmetic and copies ran while one was open for 18% -> 0% of each run, Pallas kernels for 0% -> 0%
where the time goes in v2:
time: 79.1 us; the launch traced here: 78.9 us
  Pallas kernels  76.4 us (97%)
  local copies, waits for them, and re-layouts  1.87 us (2%)
    pallas_call x2, Pallas kernels, tail(): pl.pallas_call(functools.partial(tail_kernel, layer, last), in_specs=[hbm...  50.6 us
    pallas_call x2, Pallas kernels, attention(): pl.pallas_call(functools.partial(attn_kernel, layer, prev is not None), i...  25.8 us
    unnamed x1, local copies, waits for them, and re-layouts  1.87 us

profile of v2, /device:TPU:1, one launch (start us, length us, event | category | flops | bytes accessed | tf_op | source)
XLA Modules:
  0.0 78.9 jit_solution(12172062239830277962)
XLA Ops:
  0.6 13.1 %attention_0.1 = (bf16[2,256,2,64,128]{4,3,2,1,0:T(8,128)(2,1)}, bf16[2,256,2,64,128]{4,3,2,1,0:T(8,128)(2,1)}, bf16[256,128]{1,0:T(8,128)(2,1)}) custom-call(s32[256]{0:T(256)} %len_hbm.3, f32[2,2,1024]{2,1,0:T(2,128)} %gain_hbm.7, f32[2,2,1024]{2,1,0:T(2,128)} %bias_hbm.7, bf16[2,3,2,64]{3,2,1,0:T(2,128)(2,1)} %bq_hbm.3, bf16[256,1024]{1,0:T(8,128)(2,1)} %x_hbm.1, ...), custom_call_target="tpu_custom_call" | custom-call | flops 1000000000 | bytes 33554432 | tf_op jit(solution)/shard_map/attention_0/pallas_call | solution.py:157
  13.7 26.5 %tail_0.1 = (bf16[256,1024]{1,0:T(8,128)(2,1)}, bf16[32,1024]{1,0:T(8,128)(2,1)}) custom-call(bf16[256,128]{1,0:T(8,128)(2,1)} %get-tuple-element.11.a_hbm, bf16[256,1024]{1,0:T(8,128)(2,1)} %x_hbm.1, f32[2,2,1024]{2,1,0:T(2,128)} %gain_hbm.7, f32[2,2,1024]{2,1,0:T(2,128)} %bias_hbm.7, bf16[2,1024]{1,0:T(2,128)(2,1)} %bo_hbm.3, bf16[2,512]{1,0:T(2,128)(2,1)} %bu_hbm.3, ...), custom_call_target="tpu_custom_call" | custom-call | flops 1000000000 | bytes 4194304 | tf_op jit(solution)/shard_map/tail_0/pallas_call | solution.py:325
  40.2 12.7 %attention_1.1 = (bf16[2,256,2,64,128]{4,3,2,1,0:T(8,128)(2,1)}, bf16[2,256,2,64,128]{4,3,2,1,0:T(8,128)(2,1)}, bf16[256,128]{1,0:T(8,128)(2,1)}) custom-call(s32[256]{0:T(256)} %len_hbm.3, f32[2,2,1024]{2,1,0:T(2,128)} %gain_hbm.7, f32[2,2,1024]{2,1,0:T(2,128)} %bias_hbm.7, ...), custom_call_target="tpu_custom_call", output_to_operand_aliasing={{0}: (8, {}), {1}: (9, {})} | custom-call | flops 1000000000 | bytes 33554432 | tf_op jit(solution)/shard_map/attention_1/pallas_call | solution.py:157
  52.9 24.2 %tail_1.1 = bf16[256,1024]{1,0:T(8,128)(2,1)} custom-call(bf16[256,128]{1,0:T(8,128)(2,1)} %get-tuple-element.15.a_hbm, bf16[32,1024]{1,0:T(8,128)(2,1)} %get-tuple-element.16.x_hbm, f32[2,2,1024]{2,1,0:T(2,128)} %gain_hbm.7, f32[2,2,1024]{2,1,0:T(2,128)} %bias_hbm.7, bf16[2,1024]{1,0:T(2,128)(2,1)} %bo_hbm.3, bf16[2,512]{1,0:T(2,128)(2,1)} %bu_hbm.3, ...), custom_call_target="tpu_custom_call" | custom-call | flops 1000000000 | bytes 4194304 | tf_op jit(solution)/shard_map/tail_1/pallas_call | solution.py:325
  77.1 1.9 %copy.22 = bf16[256,1024]{1,0:T(8,128)(2,1)} copy(bf16[256,1024]{1,0:T(8,128)(2,1)} %tail_1.1) | data formatting | bytes 1048576

commit v3 on v2

--- a/solution.py
+++ b/solution.py
@@ -173,6 +173,9 @@
     )(*operands)
 
 
+PIECES = 2
+
+
 def tail_kernel(layer, last, a_hbm, x_hbm, gain_hbm, bias_hbm, bo_hbm, bu_hbm, bd_hbm, wo_hbm, wu_hbm, wd_hbm, *rest):
     if last:
         out_hbm, *rest = rest
@@ -186,6 +189,8 @@
     chip = lax.div(me, 2)
     half = nb // 2
     cut = nb // 8
+    piece = cut // PIECES
+    pieces = range(PIECES)
     far = (3, 1, 2)
 
     def chip_at(dist):
@@ -199,8 +204,11 @@
     def send(src, dst, s_sem, r_sem, dev):
         return pltpu.make_async_remote_copy(src, dst, s_sem, r_sem, device_id={"tp": dev}, device_id_type=MESH)
 
-    def slot(d):
-        return pl.ds(pl.multiple_of(chip_at(d) * cut, cut), cut)
+    def slot(d, s):
+        return pl.ds(pl.multiple_of(chip_at(d) * cut + s * piece, piece), piece)
+
+    def at(s):
+        return pl.ds(s * piece, piece)
 
     row0 = pl.multiple_of(core * half + chip * cut, cut)
     x_mine = x_hbm.at[pl.ds(row0, cut)] if layer == 0 else x_hbm
@@ -217,33 +225,46 @@
         cp.wait()
     dsend[...] = jnp.dot(a_s[pl.ds(pl.multiple_of((1 - core) * half, half), half), :], wo[...], preferred_element_type=F32).astype(BF16)
     pl.semaphore_wait(barrier, 4)
-    d2d = {d: send(dsend.at[slot(d)], drecv.at[slot(d)], ds_sem.at[n], dr_sem.at[n], sibling) for n, d in enumerate(far + (0,))}
-    for d in far + (0,):
-        d2d[d].start()
+    d2d = {(s, d): send(dsend.at[slot(d, s)], drecv.at[slot(d, s)], ds_sem.at[s, n], dr_sem.at[s, n], sibling)
+           for s in pieces for n, d in enumerate(far + (0,))}
+    for cp in d2d.values():
+        cp.start()
     swap = [send(src, dst, xs_sem.at[n], xr_sem.at[n], sibling)
             for n, (src, dst) in enumerate(((bu_hbm, bu_x), (wu_hbm.at[layer], wu_x), (wd_hbm.at[layer], wd_x)))]
     for cp in swap:
         cp.start()
     own[...] = jnp.dot(a_s[pl.ds(pl.multiple_of(core * half, half), half), :], wo[...], preferred_element_type=F32)
     sends = {}
-    for n, d in enumerate(far):
-        d2d[d].wait_recv()
-        csend[0, n] = (own[slot(d), :] + drecv[slot(d), :].astype(F32)).astype(BF16)
-        sends[0, d] = send(csend.at[0, n], crecv.at[0, n], cs_sem.at[0, n], cr_sem.at[0, n], peers[d])
-        sends[0, d].start()
-    d2d[0].wait_recv()
-    total = own[slot(0), :] + drecv[slot(0), :].astype(F32)
+
+    def reduce_to(r, s, d, part):
+        n = far.index(d)
+        csend[r, n, at(s), :] = part.astype(BF16)
+        sends[r, s, d] = send(csend.at[r, n, at(s)], crecv.at[r, n, at(s)], cs_sem.at[r, s, n], cr_sem.at[r, s, n], peers[d])
+        sends[r, s, d].start()
+
+    def received(r, s, total):
+        for d in (2, 3, 1):
+            sends[r, s, d].wait_recv()
+            total = total + crecv[r, far.index(d), at(s), :].astype(F32)
+        return total
+
+    for s in pieces:
+        for d in far:
+            d2d[s, d].wait_recv()
+            reduce_to(0, s, d, own[slot(d, s), :] + drecv[slot(d, s), :].astype(F32))
     for cp in loads[2:]:
         cp.wait()
-    for n, d in ((2, 2), (1, 1), (0, 3)):
-        sends[0, d].wait_recv()
-        total = total + crecv[0, n].astype(F32)
-    xmid = (xs[...].astype(F32) + total + bo_ref[...].astype(F32)[layer:layer + 1]).astype(BF16)
-
-    hb[slot(0), :] = norm_rows(xmid.astype(F32), gain_ref[layer, 1:2, :], bias_ref[layer, 1:2, :])
-    hsend = {d: send(hb.at[slot(0)], hb.at[slot(0)], hs_sem.at[n], hr_sem.at[n], peers[d]) for n, d in enumerate(far)}
-    for d in far:
-        hsend[d].start()
+    xmid, hsend = {}, {}
+    for s in pieces:
+        d2d[s, 0].wait_recv()
+        total = received(0, s, own[slot(0, s), :] + drecv[slot(0, s), :].astype(F32))
+        xmid[s] = (xs[at(s), :].astype(F32) + total + bo_ref[...].astype(F32)[layer:layer + 1]).astype(BF16)
+        mine = hb.at[slot(0, s)]
+        mine[...] = norm_rows(xmid[s].astype(F32), gain_ref[layer, 1:2, :], bias_ref[layer, 1:2, :])
+        for n, d in enumerate(far):
+            hsend[s, d] = send(mine, mine, hs_sem.at[s, n], hr_sem.at[s, n], peers[d])
+            hsend[s, d].start()
+
     for cp in swap:
         cp.wait_recv()
 
@@ -255,58 +276,55 @@
             part = y if part is None else part + y
         return part
 
-    def arrived(d):
-        n = far.index(d)
-        send(hb.at[slot(0)], hb.at[slot(d)], hs_sem.at[n], hr_sem.at[n], peers[d]).wait_recv()
-
-    total = mlp(hb[slot(0), :])
-    for together in ((2, 3), (1,)):
-        for d in together:
-            arrived(d)
-        part = mlp(jnp.concatenate([hb[slot(d), :] for d in together], axis=0))
-        for i, d in sorted(enumerate(together), key=lambda t: -t[1]):
+    own[0:cut, :] = mlp(jnp.concatenate([hb[slot(0, s), :] for s in pieces], axis=0))
+    for s in pieces:
+        for n, d in enumerate(far):
+            send(hb.at[slot(0, s)], hb.at[slot(d, s)], hs_sem.at[s, n], hr_sem.at[s, n], peers[d]).wait_recv()
+        part = mlp(jnp.concatenate([hb[slot(d, s), :] for d in far], axis=0))
+        for n, d in enumerate(far):
+            reduce_to(1, s, d, part[n * piece:(n + 1) * piece])
+
+    def place(d, k, s):
+        return pl.ds(pl.multiple_of(k * half + chip_at(d) * cut + s * piece, piece), piece)
+
+    kept = []
+
+    def keep(d, k, s, n):
+        kept.append(pltpu.make_async_copy(ob.at[place(d, k, s)], out_hbm.at[place(d, k, s)], o_sem.at[s, n]))
+        kept[-1].start()
+
+    spread = {}
+    for s in pieces:
+        total = received(1, s, own[at(s), :])
+        xnew = (xmid[s].astype(F32) + total + bd_ref[...].astype(F32)[layer:layer + 1]).astype(BF16)
+        mine = ob.at[place(0, core, s)]
+        if last:
+            mine[...] = xnew
+        else:
+            mine[...] = norm_rows(xnew.astype(F32), gain_ref[layer + 1, 0:1, :], bias_ref[layer + 1, 0:1, :])
+        for n, (d, dev) in enumerate([(d, peers[d]) for d in far] + [(0, sibling)]):
+            spread[s, d] = send(mine, mine, gs_sem.at[s, n], gr_sem.at[s, n], dev)
+            spread[s, d].start()
+        keep(0, core, s, 0)
+        if not last:
+            xs[at(s), :] = xnew
+            kept.append(pltpu.make_async_copy(xs.at[at(s)], xrow_out.at[at(s)], o_sem.at[s, 8]))
+            kept[-1].start()
+    passed = {}
+    for s in pieces:
+        for d in (2, 3, 1):
             n = far.index(d)
-            csend[1, n] = part[i * cut:(i + 1) * cut].astype(BF16)
-            sends[1, d] = send(csend.at[1, n], crecv.at[1, n], cs_sem.at[1, n], cr_sem.at[1, n], peers[d])
-            sends[1, d].start()
-    for n, d in ((2, 2), (0, 3), (1, 1)):
-        sends[1, d].wait_recv()
-        total = total + crecv[1, n].astype(F32)
-    xnew = (xmid.astype(F32) + total + bd_ref[...].astype(F32)[layer:layer + 1]).astype(BF16)
-
-    def block(d, k):
-        return ob.at[pl.ds(pl.multiple_of(k * half + chip_at(d) * cut, cut), cut)]
-
-    def keep(d, k, n):
-        cp = pltpu.make_async_copy(block(d, k), out_hbm.at[pl.ds(pl.multiple_of(k * half + chip_at(d) * cut, cut), cut)], o_sem.at[n])
-        cp.start()
-        return cp
-
-    mine = block(0, core)
-    if last:
-        mine[...] = xnew
-    else:
-        mine[...] = norm_rows(xnew.astype(F32), gain_ref[layer + 1, 0:1, :], bias_ref[layer + 1, 0:1, :])
-    spread = {d: send(mine, mine, gs_sem.at[n], gr_sem.at[n], dev) for n, (d, dev) in enumerate([(d, peers[d]) for d in far] + [(0, sibling)])}
-    for d in far + (0,):
-        spread[d].start()
-    kept = [keep(0, core, 0)]
-    if not last:
-        xs[...] = xnew
-        kept.append(pltpu.make_async_copy(xs, xrow_out, o_sem.at[8]))
-        kept[-1].start()
-    passed = {}
-    for d in (2, 3, 1):
-        n = far.index(d)
-        send(mine, block(d, core), gs_sem.at[n], gr_sem.at[n], peers[d]).wait_recv()
-        passed[d] = send(block(d, core), block(d, core), gs_sem.at[4 + n], gr_sem.at[4 + n], sibling)
-        passed[d].start()
-        kept.append(keep(d, core, 1 + n))
-    spread[0].wait_recv()
-    kept.append(keep(0, 1 - core, 4))
-    for d in (2, 3, 1):
-        passed[d].wait_recv()
-        kept.append(keep(d, 1 - core, 5 + far.index(d)))
+            block = ob.at[place(d, core, s)]
+            send(ob.at[place(0, core, s)], block, gs_sem.at[s, n], gr_sem.at[s, n], peers[d]).wait_recv()
+            passed[s, d] = send(block, block, gs_sem.at[s, 4 + n], gr_sem.at[s, 4 + n], sibling)
+            passed[s, d].start()
+            keep(d, core, s, 1 + n)
+    for s in pieces:
+        spread[s, 0].wait_recv()
+        keep(0, 1 - core, s, 4)
+        for d in (2, 3, 1):
+            passed[s, d].wait_recv()
+            keep(d, 1 - core, s, 5 + far.index(d))
     for cp in [*d2d.values(), *swap, *sends.values(), *hsend.values(), *spread.values(), *passed.values()]:
         cp.wait_send()
     for cp in kept:
@@ -336,8 +354,8 @@
             pltpu.VMEM((half, width), BF16), pltpu.VMEM((nb, width), BF16), pltpu.VMEM((half, width), F32),
             pltpu.VMEM((half, width), BF16), pltpu.VMEM((half, width), BF16),
             pltpu.VMEM((2, 3, cut, width), BF16), pltpu.VMEM((2, 3, cut, width), BF16),
-            dma((10,)), dma((9,)), dma((3,)), dma((3,)), dma((4,)), dma((4,)),
-            dma((2, 3)), dma((2, 3)), dma((3,)), dma((3,)), dma((7,)), dma((7,))],
+            dma((10,)), dma((PIECES, 9)), dma((3,)), dma((3,)), dma((PIECES, 4)), dma((PIECES, 4)),
+            dma((2, PIECES, 3)), dma((2, PIECES, 3)), dma((PIECES, 3)), dma((PIECES, 3)), dma((PIECES, 7)), dma((PIECES, 7))],
         compiler_params=pltpu.CompilerParams(collective_id=layer, has_side_effects=True, vmem_limit_bytes=ATTN_VMEM),
         cost_estimate=pl.CostEstimate(flops=10 ** 9, bytes_accessed=2 ** 22, transcendentals=0),
         name=f"tail_{layer}",

time: 79.1 us -> 75 us (0.948)
  Pallas kernels: 76.4 us -> 72.3 us
    pallas_call x2, Pallas kernels: 50.6 us -> 46.5 us  [tail(): pl.pallas_call(functools.partial(tail_kernel, layer, last), in_specs=[hbm...]
where the time goes in v3:
time: 75 us; the launch traced here: 74.8 us
  Pallas kernels  72.3 us (96%)
  local copies, waits for them, and re-layouts  1.87 us (2%)
    pallas_call x2, Pallas kernels, tail(): pl.pallas_call(functools.partial(tail_kernel, layer, last), in_specs=[hbm...  46.5 us
    pallas_call x2, Pallas kernels, attention(): pl.pallas_call(functools.partial(attn_kernel, layer, prev is not None), i...  25.7 us
    unnamed x1, local copies, waits for them, and re-layouts  1.87 us

profile of v3, /device:TPU:1, one launch (start us, length us, event | category | flops | bytes accessed | tf_op | source)
XLA Modules:
  0.0 74.8 jit_solution(13395848624979331778)
XLA Ops:
  0.6 13.1 %attention_0.1 = (bf16[2,256,2,64,128]{4,3,2,1,0:T(8,128)(2,1)}, bf16[2,256,2,64,128]{4,3,2,1,0:T(8,128)(2,1)}, bf16[256,128]{1,0:T(8,128)(2,1)}) custom-call(s32[256]{0:T(256)} %len_hbm.3, f32[2,2,1024]{2,1,0:T(2,128)} %gain_hbm.7, f32[2,2,1024]{2,1,0:T(2,128)} %bias_hbm.7, bf16[2,3,2,64]{3,2,1,0:T(2,128)(2,1)} %bq_hbm.3, bf16[256,1024]{1,0:T(8,128)(2,1)} %x_hbm.1, ...), custom_call_target="tpu_custom_call" | custom-call | flops 1000000000 | bytes 33554432 | tf_op jit(solution)/shard_map/attention_0/pallas_call | solution.py:157
  13.7 24.9 %tail_0.1 = (bf16[256,1024]{1,0:T(8,128)(2,1)}, bf16[32,1024]{1,0:T(8,128)(2,1)}) custom-call(bf16[256,128]{1,0:T(8,128)(2,1)} %get-tuple-element.11.a_hbm, bf16[256,1024]{1,0:T(8,128)(2,1)} %x_hbm.1, f32[2,2,1024]{2,1,0:T(2,128)} %gain_hbm.7, f32[2,2,1024]{2,1,0:T(2,128)} %bias_hbm.7, bf16[2,1024]{1,0:T(2,128)(2,1)} %bo_hbm.3, bf16[2,512]{1,0:T(2,128)(2,1)} %bu_hbm.3, ...), custom_call_target="tpu_custom_call" | custom-call | flops 1000000000 | bytes 4194304 | tf_op jit(solution)/shard_map/tail_0/pallas_call | solution.py:343
  38.7 12.6 %attention_1.1 = (bf16[2,256,2,64,128]{4,3,2,1,0:T(8,128)(2,1)}, bf16[2,256,2,64,128]{4,3,2,1,0:T(8,128)(2,1)}, bf16[256,128]{1,0:T(8,128)(2,1)}) custom-call(s32[256]{0:T(256)} %len_hbm.3, f32[2,2,1024]{2,1,0:T(2,128)} %gain_hbm.7, f32[2,2,1024]{2,1,0:T(2,128)} %bias_hbm.7, ...), custom_call_target="tpu_custom_call", output_to_operand_aliasing={{0}: (8, {}), {1}: (9, {})} | custom-call | flops 1000000000 | bytes 33554432 | tf_op jit(solution)/shard_map/attention_1/pallas_call | solution.py:157
  51.3 21.6 %tail_1.1 = bf16[256,1024]{1,0:T(8,128)(2,1)} custom-call(bf16[256,128]{1,0:T(8,128)(2,1)} %get-tuple-element.15.a_hbm, bf16[32,1024]{1,0:T(8,128)(2,1)} %get-tuple-element.16.x_hbm, f32[2,2,1024]{2,1,0:T(2,128)} %gain_hbm.7, f32[2,2,1024]{2,1,0:T(2,128)} %bias_hbm.7, bf16[2,1024]{1,0:T(2,128)(2,1)} %bo_hbm.3, bf16[2,512]{1,0:T(2,128)(2,1)} %bu_hbm.3, ...), custom_call_target="tpu_custom_call" | custom-call | flops 1000000000 | bytes 4194304 | tf_op jit(solution)/shard_map/tail_1/pallas_call | solution.py:343
  72.9 1.9 %copy.22 = bf16[256,1024]{1,0:T(8,128)(2,1)} copy(bf16[256,1024]{1,0:T(8,128)(2,1)} %tail_1.1) | data formatting | bytes 1048576

commit v4 on v3

--- a/solution.py
+++ b/solution.py
@@ -13,7 +13,9 @@
 MESH = pl.DeviceIdType.MESH
 GB = 32
 ATTN_VMEM = 63 * 2 ** 20
-EARLY = 4
+READS = ((0, 1), (1, 2), (2, 4), (4, 6), (6, 8))
+WRITES = (((0, 2), (2, 4), (4, 6), (6, 7), (7, 8)), ((0, 1), (1, 3), (3, 5), (5, 7), (7, 8)))
+EARLY = 3
 
 
 def norm_rows(xf, gain, bias):
@@ -39,15 +41,18 @@
     def rows(g):
         return pl.ds(g * GB, GB)
 
-    def load(g):
-        return [pltpu.make_async_copy(hbm.at[layer, rows(g)], buf.at[rows(g)], in_sem.at[t, g])
+    def part(piece):
+        return pl.ds(piece[0] * GB, (piece[1] - piece[0]) * GB)
+
+    def load(piece):
+        return [pltpu.make_async_copy(hbm.at[layer, part(piece)], buf.at[part(piece)], in_sem.at[t, piece[0]])
                 for t, (hbm, buf) in enumerate(((k_hbm, k_s), (v_hbm, v_s)))]
 
     def save_a(g):
         return pltpu.make_async_copy(a_ref.at[rows(g)], a_out.at[rows(g)], a_sem.at[g])
 
-    def save(g):
-        return [pltpu.make_async_copy(buf.at[rows(g)], hbm.at[layer, rows(g)], out_sem.at[t, g])
+    def save(piece):
+        return [pltpu.make_async_copy(buf.at[part(piece)], hbm.at[layer, part(piece)], out_sem.at[t, piece[0]])
                 for t, (hbm, buf) in enumerate(((k_out, k_s), (v_out, v_s)))]
 
     pairs = [(x_in, h_s), (w_hbm.at[layer], w_s), (bq_hbm, bq_ref), (len_hbm, len_ref)]
@@ -56,13 +61,13 @@
     first = [pltpu.make_async_copy(src, dst, first_sem.at[i]) for i, (src, dst) in enumerate(pairs)]
     for cp in first:
         cp.start()
-    for g in range(EARLY):
-        for cp in load(g):
+    for piece in READS[:EARLY]:
+        for cp in load(piece):
             cp.start()
     for cp in first:
         cp.wait()
-    for g in range(EARLY, groups):
-        for cp in load(g):
+    for piece in READS[EARLY:]:
+        for cp in load(piece):
             cp.start()
     if layer == 0:
         for r in range(0, nb, 64):
@@ -127,8 +132,10 @@
     lens, p = {}, {}
     for g in range(groups + 2):
         if g < groups:
-            for cp in load(g):
-                cp.wait()
+            for piece in READS:
+                if piece[0] == g:
+                    for cp in load(piece):
+                        cp.wait()
             lens[g] = [len_ref[g * GB + i] for i in range(GB)]
         if g >= 2:
             weigh(g - 2, p.pop(g - 2))
@@ -136,11 +143,15 @@
             p[g - 1] = probs(g - 1, lens[g - 1])
         if g < groups:
             insert(g, lens[g])
-            for cp in save(g):
-                cp.start()
+            for piece in WRITES[layer % 2]:
+                if piece[1] == g + 1:
+                    for cp in save(piece):
+                        cp.start()
+    for piece in WRITES[layer % 2]:
+        for cp in save(piece):
+            cp.wait()
     for g in range(groups):
-        for cp in save(g) + [save_a(g)]:
-            cp.wait()
+        save_a(g).wait()
 
 
 def attention(layer, cache_len, x, gain, bias, w_t, b_qkv, k_t, v_t, prev):

time: 75 us -> 73.5 us (0.980)
  Pallas kernels: 72.3 us -> 70.8 us
    pallas_call x2, Pallas kernels: 25.7 us -> 24.3 us  [attention(): pl.pallas_call(functools.partial(attn_kernel, layer, prev is not None), i...]
where the time goes in v4:
time: 73.5 us; the launch traced here: 73.3 us
  Pallas kernels  70.8 us (96%)
  local copies, waits for them, and re-layouts  1.87 us (3%)
    pallas_call x2, Pallas kernels, tail(): pl.pallas_call(functools.partial(tail_kernel, layer, last), in_specs=[hbm...  46.5 us
    pallas_call x2, Pallas kernels, attention(): pl.pallas_call(functools.partial(attn_kernel, layer, prev is not None), i...  24.3 us
    unnamed x1, local copies, waits for them, and re-layouts  1.87 us

profile of v4, /device:TPU:1, one launch (start us, length us, event | category | flops | bytes accessed | tf_op | source)
XLA Modules:
  0.0 73.3 jit_solution(173691251145124895)
XLA Ops:
  0.6 12.3 %attention_0.1 = (bf16[2,256,2,64,128]{4,3,2,1,0:T(8,128)(2,1)}, bf16[2,256,2,64,128]{4,3,2,1,0:T(8,128)(2,1)}, bf16[256,128]{1,0:T(8,128)(2,1)}) custom-call(s32[256]{0:T(256)} %len_hbm.3, f32[2,2,1024]{2,1,0:T(2,128)} %gain_hbm.7, f32[2,2,1024]{2,1,0:T(2,128)} %bias_hbm.7, bf16[2,3,2,64]{3,2,1,0:T(2,128)(2,1)} %bq_hbm.3, bf16[256,1024]{1,0:T(8,128)(2,1)} %x_hbm.1, ...), custom_call_target="tpu_custom_call" | custom-call | flops 1000000000 | bytes 33554432 | tf_op jit(solution)/shard_map/attention_0/pallas_call | solution.py:168
  12.9 24.9 %tail_0.1 = (bf16[256,1024]{1,0:T(8,128)(2,1)}, bf16[32,1024]{1,0:T(8,128)(2,1)}) custom-call(bf16[256,128]{1,0:T(8,128)(2,1)} %get-tuple-element.11.a_hbm, bf16[256,1024]{1,0:T(8,128)(2,1)} %x_hbm.1, f32[2,2,1024]{2,1,0:T(2,128)} %gain_hbm.7, f32[2,2,1024]{2,1,0:T(2,128)} %bias_hbm.7, bf16[2,1024]{1,0:T(2,128)(2,1)} %bo_hbm.3, bf16[2,512]{1,0:T(2,128)(2,1)} %bu_hbm.3, ...), custom_call_target="tpu_custom_call" | custom-call | flops 1000000000 | bytes 4194304 | tf_op jit(solution)/shard_map/tail_0/pallas_call | solution.py:354
  37.9 12.0 %attention_1.1 = (bf16[2,256,2,64,128]{4,3,2,1,0:T(8,128)(2,1)}, bf16[2,256,2,64,128]{4,3,2,1,0:T(8,128)(2,1)}, bf16[256,128]{1,0:T(8,128)(2,1)}) custom-call(s32[256]{0:T(256)} %len_hbm.3, f32[2,2,1024]{2,1,0:T(2,128)} %gain_hbm.7, f32[2,2,1024]{2,1,0:T(2,128)} %bias_hbm.7, ...), custom_call_target="tpu_custom_call", output_to_operand_aliasing={{0}: (8, {}), {1}: (9, {})} | custom-call | flops 1000000000 | bytes 33554432 | tf_op jit(solution)/shard_map/attention_1/pallas_call | solution.py:168
  49.8 21.6 %tail_1.1 = bf16[256,1024]{1,0:T(8,128)(2,1)} custom-call(bf16[256,128]{1,0:T(8,128)(2,1)} %get-tuple-element.15.a_hbm, bf16[32,1024]{1,0:T(8,128)(2,1)} %get-tuple-element.16.x_hbm, f32[2,2,1024]{2,1,0:T(2,128)} %gain_hbm.7, f32[2,2,1024]{2,1,0:T(2,128)} %bias_hbm.7, bf16[2,1024]{1,0:T(2,128)(2,1)} %bo_hbm.3, bf16[2,512]{1,0:T(2,128)(2,1)} %bu_hbm.3, ...), custom_call_target="tpu_custom_call" | custom-call | flops 1000000000 | bytes 4194304 | tf_op jit(solution)/shard_map/tail_1/pallas_call | solution.py:354
  71.5 1.9 %copy.22 = bf16[256,1024]{1,0:T(8,128)(2,1)} copy(bf16[256,1024]{1,0:T(8,128)(2,1)} %tail_1.1) | data formatting | bytes 1048576
